TPU v7x, 32 devices: a whole 2x2x4 slice. The times are simulated.
32 devices in a mesh: dp: 8 (over z, y), seq: 4 (over x, core).
Axes of the slice: x: 2, y: 2, z: 4, core: 2. Of those that a mesh axis runs over, the one named last changes fastest.
Arguments:
- layer_input: bfloat16 [8, 512, 2048], P('dp', 'seq'), may hold values from -6 to 6
- writes_first: bfloat16 [8, 512, 128], P('dp', 'seq'), may hold values from -0.375 to 0.375
- reads_first: bfloat16 [8, 512, 128], P('dp', 'seq'), may hold values from -0.375 to 0.375
- decay_first: float32 [8, 32, 512], P('dp', None, 'seq'), may hold values from -1.5 to 0, as said below
- skip_first: float32 [32], replicated, may hold values from 0.5 to 1.5
- writes_second: bfloat16 [8, 512, 128], P('dp', 'seq'), may hold values from -0.375 to 0.375
- reads_second: bfloat16 [8, 512, 128], P('dp', 'seq'), may hold values from -0.375 to 0.375
- decay_second: float32 [8, 32, 512], P('dp', None, 'seq'), may hold values from -1.5 to 0, as said below
- skip_second: float32 [32], replicated, may hold values from 0.5 to 1.5
- order_first: int32 [512], P('seq'), may hold values from 0 to 511, as said below
- order_second: int32 [512], P('seq'), may hold values from 0 to 511, as said below
- cotangent: float32 [8, 512, 2048], P('dp', 'seq'), may hold values from -48 to 48
Outputs:
- grad_input: bfloat16 [8, 512, 2048], P('dp', 'seq')
- grad_writes_first: bfloat16 [8, 512, 128], P('dp', 'seq')
- grad_reads_first: bfloat16 [8, 512, 128], P('dp', 'seq')
- grad_decay_first: float32 [8, 32, 512], P('dp', None, 'seq')
- grad_skip_first: float32 [32], replicated
- grad_writes_second: bfloat16 [8, 512, 128], P('dp', 'seq')
- grad_reads_second: bfloat16 [8, 512, 128], P('dp', 'seq')
- grad_decay_second: float32 [8, 32, 512], P('dp', None, 'seq')
- grad_skip_second: float32 [32], replicated
Inputs may be any that keep to these rules, and one draw needn't show every extreme that they name: order_first lists the cells of a 16 by 32 grid (cell i * 32 + j for row i, column j) row after row from row 0 on, each row left to right or right to left. order_second lists the same cells column after column from column 0 on, each column top to bottom or bottom to top. `decay_first`: every entry is negative. `decay_second`: every entry is negative.
All inputs are finite; a program needn't handle non-finite values.
Results may differ from a plain program's by a relative error of at most 0.005.
Values may be sent and summed in bfloat16 or wider, within the bound.
A program may use at most 128 MiB of HBM per device.

v0:
```python
import functools
import math

import jax
import jax.numpy as jnp
from jax import lax
from jax.experimental import pallas as pl
from jax.experimental.pallas import tpu as pltpu
from jax.sharding import PartitionSpec as P

MESH = pl.DeviceIdType.MESH
HIGHEST = lax.Precision.HIGHEST
F32 = jnp.float32
BF16 = jnp.bfloat16


def nn(a, b, precision=None):
    return lax.dot_general(a, b, (((1,), (0,)), ((), ())), precision=precision, preferred_element_type=F32)


def nt(a, b, precision=None):
    return lax.dot_general(a, b, (((1,), (1,)), ((), ())), precision=precision, preferred_element_type=F32)


def tn(a, b, precision=None):
    return lax.dot_general(a, b, (((0,), (0,)), ((), ())), precision=precision, preferred_element_type=F32)


def iota(shape, dim):
    return lax.broadcasted_iota(jnp.int32, shape, dim)


def exchange_in_kernel(n, heads, *refs):
    (u, w1, r1, w2, r2, g1, g2, o1, o2, ct) = refs[:10]
    (u_all, w1_all, r1_all, w2_all, r2_all, g1_all, g2_all, o1_all, o2_all, ct_all) = refs[10:20]
    ct_low, send, recv = refs[20:]
    me = lax.axis_index("seq")
    width = u.shape[1] // n
    barrier = pltpu.get_barrier_semaphore()
    for d in range(1, n):
        pl.semaphore_signal(barrier, inc=1, device_id={"seq": lax.rem(me + d, n)}, device_id_type=MESH)
    ct_low[...] = ct[...].astype(BF16)
    pl.semaphore_wait(barrier, n - 1)

    def cut(ref, at):
        return ref.at[:, pl.ds(pl.multiple_of(at * width, width), width)]

    copies = []
    for d in range(1, n):
        to = lax.rem(me + d, n)
        pairs = [
            (g1.at[to], g1_all.at[me]),
            (g2.at[to], g2_all.at[me]),
            (w1, w1_all.at[me]),
            (r1, r1_all.at[me]),
            (w2, w2_all.at[me]),
            (r2, r2_all.at[me]),
            (o1, o1_all.at[me]),
            (o2, o2_all.at[me]),
            (cut(u, to), u_all.at[me]),
            (cut(ct_low, to), ct_all.at[me]),
        ]
        for k, (src, dst) in enumerate(pairs):
            copy = pltpu.make_async_remote_copy(
                src_ref=src,
                dst_ref=dst,
                send_sem=send.at[d - 1, k],
                recv_sem=recv.at[d - 1, k],
                device_id={"seq": to},
                device_id_type=MESH,
            )
            copy.start()
            copies.append(copy)
    g1_all[me] = g1[me]
    g2_all[me] = g2[me]
    w1_all[me] = w1[...]
    r1_all[me] = r1[...]
    w2_all[me] = w2[...]
    r2_all[me] = r2[...]
    o1_all[me] = o1[...]
    o2_all[me] = o2[...]
    here = pl.ds(pl.multiple_of(me * width, width), width)
    u_all[me] = u[:, here]
    ct_all[me] = ct_low[:, here]
    for copy in copies:
        copy.wait()


def exchange_in(n, u, w1, r1, w2, r2, g1, g2, o1, o2, ct):
    length, features = u.shape
    heads = g1.shape[1]

    def out(*shape, dtype):
        return jax.ShapeDtypeStruct((n,) + shape, dtype)

    states = w1.shape[1]
    vmem = pl.BlockSpec(memory_space=pltpu.VMEM)
    return pl.pallas_call(
        functools.partial(exchange_in_kernel, n, heads),
        out_shape=(
            out(length, features // n, dtype=BF16),
            out(length, states, dtype=BF16),
            out(length, states, dtype=BF16),
            out(length, states, dtype=BF16),
            out(length, states, dtype=BF16),
            out(heads, length, dtype=F32),
            out(heads, length, dtype=F32),
            out(1, length, dtype=jnp.int32),
            out(1, length, dtype=jnp.int32),
            out(length, features // n, dtype=BF16),
        ),
        in_specs=[vmem] * 10,
        out_specs=[vmem] * 10,
        scratch_shapes=[
            pltpu.VMEM((length, features), BF16),
            pltpu.SemaphoreType.DMA((n - 1, 10)),
            pltpu.SemaphoreType.DMA((n - 1, 10)),
        ],
        compiler_params=pltpu.CompilerParams(collective_id=0, has_side_effects=True),
        name="exchange_in",
    )(u, w1, r1, w2, r2, g1, g2, o1, o2, ct)


def spread(x, size):
    per = 128 // size
    rows, heads = x.shape
    lane = iota((rows, 128), 1) // size
    parts = []
    for j in range(heads // per):
        part = jnp.broadcast_to(x[:, per * j : per * j + 1], (rows, 128))
        for k in range(1, per):
            part = jnp.where(lane == k, x[:, per * j + k : per * j + k + 1], part)
        parts.append(part)
    return jnp.concatenate(parts, axis=1)


def split_heads(x, size):
    lane = iota(x.shape, 1) // size
    return jnp.concatenate([jnp.where(lane == k, x, jnp.zeros_like(x)) for k in range(128 // size)], axis=0)


def scale_rows(state, factor, size):
    heads = factor.shape[0]
    return jnp.concatenate(
        [state[h * size : (h + 1) * size] * factor[h : h + 1] for h in range(heads)], axis=0
    )


class Chunk:
    def __init__(self, log_decay, size):
        heads, length = log_decay.shape
        self.size, self.heads, self.length = size, heads, length
        before = (iota((length, length), 0) <= iota((length, length), 1)).astype(F32)
        after = (iota((length, length), 1) <= iota((length, length), 0)).astype(F32)
        self.row = nn(log_decay, before, HIGHEST)
        self.col = nt(after, log_decay, HIGHEST)
        total = self.col[length - 1 : length, :]
        self.grown = jnp.exp(self.col)
        self.left = jnp.exp(total - self.col)
        self.total = jnp.exp(self.row[:, length - 1 : length])

    def gaps(self, h):
        gap = self.col[:, h : h + 1] - self.row[h : h + 1, :]
        causal = iota(gap.shape, 0) >= iota(gap.shape, 1)
        return jnp.where(causal, jnp.exp(jnp.minimum(gap, 0.0)), 0.0)

    def gaps_turned(self, h):
        gap = self.row[h : h + 1, :] - self.col[:, h : h + 1]
        causal = iota(gap.shape, 0) <= iota(gap.shape, 1)
        return jnp.where(causal, jnp.exp(jnp.minimum(gap, 0.0)), 0.0)


def layer_forward(u, w, r, chunk, skip, state):
    size = chunk.size
    per = 128 // size
    scores = nt(r, w)
    outputs = []
    for j in range(chunk.heads // per):
        weights = jnp.concatenate(
            [(chunk.gaps(per * j + k) * scores).astype(BF16) for k in range(per)], axis=1
        )
        outputs.append(nn(weights, split_heads(u[:, 128 * j : 128 * (j + 1)], size)))
    wide = u.astype(F32)
    y = jnp.concatenate(outputs, axis=1) + spread(chunk.grown, size) * nt(r, state.astype(BF16)) + skip * wide
    scaled = (wide * spread(chunk.left, size)).astype(BF16)
    return y, scale_rows(state, chunk.total, size) + tn(scaled, w)


def layer_back(dy, w, r, chunk, skip, adjoint):
    size = chunk.size
    per = 128 // size
    scores = nt(w, r)
    outputs = []
    for j in range(chunk.heads // per):
        weights = jnp.concatenate(
            [(chunk.gaps_turned(per * j + k) * scores).astype(BF16) for k in range(per)], axis=1
        )
        outputs.append(nn(weights, split_heads(dy[:, 128 * j : 128 * (j + 1)], size)))
    wide = dy.astype(F32)
    du = jnp.concatenate(outputs, axis=1) + spread(chunk.left, size) * nt(w, adjoint.astype(BF16)) + skip * wide
    scaled = (wide * spread(chunk.grown, size)).astype(BF16)
    return du, scale_rows(adjoint, chunk.total, size) + tn(scaled, r)


def layer_grads(u, dy, w, r, chunk, skip, state, adjoint, want_input):
    size, heads, length = chunk.size, chunk.heads, chunk.length
    per = 128 // size
    features = heads * size
    scores = nt(w, r)
    since = (iota((length, length), 0) >= iota((length, length), 1)).astype(BF16)
    earlier = iota((length, length), 0) < iota((length, length), 1)
    picks = (iota((heads, features), 1) // size == iota((heads, features), 0)).astype(BF16)
    dscores = jnp.zeros((length, length), F32)
    rows, outputs = [], []
    for j in range(heads // per):
        lanes = slice(128 * j, 128 * (j + 1))
        crossed = nt(split_heads(u[:, lanes], size), dy[:, lanes])
        moved, weights = [], []
        for k in range(per):
            gap = chunk.gaps_turned(per * j + k)
            part = gap * crossed[k * length : (k + 1) * length]
            dscores = dscores + part
            moved.append((part * scores).astype(BF16))
            if want_input:
                weights.append((gap * scores).astype(BF16))
        sums = nn(jnp.concatenate(moved, axis=0), since)
        for k in range(per):
            rows.append(
                jnp.sum(
                    jnp.where(earlier, sums[k * length : (k + 1) * length], 0.0), axis=0, keepdims=True
                )
            )
        if want_input:
            outputs.append(nn(jnp.concatenate(weights, axis=1), split_heads(dy[:, lanes], size)))
    wide_u, wide_dy = u.astype(F32), dy.astype(F32)
    left = spread(chunk.left, size)
    dy_scaled = wide_dy * spread(chunk.grown, size)
    u_scaled = wide_u * left
    dy_low, u_low = dy_scaled.astype(BF16), u_scaled.astype(BF16)
    state_low, adjoint_low = state.astype(BF16), adjoint.astype(BF16)
    dscores = dscores.astype(BF16)
    dreads = tn(dscores, w) + nn(dy_low, state_low)
    dwrites = nn(dscores, r) + nn(u_low, adjoint_low)
    read = nt(r, state_low)
    back = nt(w, adjoint_low)
    come = nt(picks, (dy_scaled * read).astype(BF16))
    gone = nt(picks, (u_scaled * back).astype(BF16))
    through = jnp.sum(nn(picks, (state * adjoint).astype(BF16)), axis=1, keepdims=True) * chunk.total
    ddecay = (
        jnp.concatenate(rows, axis=0)
        + nn(come.astype(BF16), since)
        + nn(gone.astype(BF16), earlier.astype(BF16))
        + through
    )
    dskip = jnp.sum(wide_u * wide_dy, axis=0, keepdims=True)
    if want_input:
        du = jnp.concatenate(outputs, axis=1) + left * back + skip * wide_dy
        return dwrites, dreads, ddecay, dskip, du, scale_rows(adjoint, chunk.total, size) + tn(dy_low, r)
    return dwrites, dreads, ddecay, dskip, None, scale_rows(state, chunk.total, size) + tn(u_low, w)


def compute_kernel(n, size, *refs):
    (u1, w1, r1, w2, r2, g1, g2, o1, o2, ct, k1, k2) = refs[:12]
    (du1, params, decays, skips) = refs[12:16]
    (y1, du2, u2, dy1, states, adjoints, state, adjoint) = refs[16:]
    heads, length = g1.shape[1:]
    features = u1.shape[2]
    first = lax.axis_index("seq") * heads

    def gains(ref):
        channel = iota((1, features), 1) // size
        row = jnp.zeros((1, features), F32)
        for h in range(heads):
            row = jnp.where(channel == h, ref[first + h], row)
        return row

    skip1, skip2 = gains(k1), gains(k2)
    state[...] = jnp.zeros_like(state)
    adjoint[...] = jnp.zeros_like(adjoint)

    def outer(i, carry):
        b = n - 1 - i
        states[i] = state[...]
        y, new = layer_forward(u1[i], w1[i], r1[i], Chunk(g1[i], size), skip1, state[...])
        y1[i] = y.astype(BF16)
        state[...] = new
        adjoints[b] = adjoint[...]
        du, new = layer_back(ct[b], w2[b], r2[b], Chunk(g2[b], size), skip2, adjoint[...])
        du2[b] = du.astype(BF16)
        adjoint[...] = new
        return carry

    lax.fori_loop(0, n, outer, 0)

    def regrid(i, carry):
        second = jnp.transpose(jnp.broadcast_to(o2[i].astype(F32), (length, length)))
        first_cells = jnp.transpose(jnp.broadcast_to(o1[i].astype(F32), (length, length)))
        forward = jnp.zeros((length, features), F32)
        back = jnp.zeros((length, features), F32)
        for j in range(n):
            take = (second == o1[j].astype(F32)).astype(BF16)
            forward = forward + nn(take, y1[j])
            take = (first_cells == o2[j].astype(F32)).astype(BF16)
            back = back + nn(take, du2[j])
        u2[i] = forward.astype(BF16)
        dy1[i] = back.astype(BF16)
        return carry

    lax.fori_loop(0, n, regrid, 0)
    state[...] = jnp.zeros_like(state)
    adjoint[...] = jnp.zeros_like(adjoint)
    skips[...] = jnp.zeros_like(skips)

    def inner(i, carry):
        b = n - 1 - i
        dw, dr, dg, dk, _, new = layer_grads(
            u2[i], ct[i], w2[i], r2[i], Chunk(g2[i], size), skip2, state[...], adjoints[i], False
        )
        state[...] = new
        params[i, 2] = dw.astype(params.dtype)
        params[i, 3] = dr.astype(params.dtype)
        decays[i, 1] = dg
        skips[1:2, :] += dk
        dw, dr, dg, dk, du, new = layer_grads(
            u1[b], dy1[b], w1[b], r1[b], Chunk(g1[b], size), skip1, states[b], adjoint[...], True
        )
        adjoint[...] = new
        du1[b] = du.astype(BF16)
        params[b, 0] = dw.astype(params.dtype)
        params[b, 1] = dr.astype(params.dtype)
        decays[b, 0] = dg
        skips[0:1, :] += dk
        return carry

    lax.fori_loop(0, n, inner, 0)


def compute(n, size, u, w1, r1, w2, r2, g1, g2, o1, o2, ct, k1, k2):
    _, length, features = u.shape
    heads = g1.shape[1]
    states = w1.shape[2]
    vmem = pl.BlockSpec(memory_space=pltpu.VMEM)
    smem = pl.BlockSpec(memory_space=pltpu.SMEM)
    return pl.pallas_call(
        functools.partial(compute_kernel, n, size),
        out_shape=(
            jax.ShapeDtypeStruct((n, length, features), BF16),
            jax.ShapeDtypeStruct((n, 4, length, states), BF16),
            jax.ShapeDtypeStruct((n, 2, heads, length), F32),
            jax.ShapeDtypeStruct((2, features), F32),
        ),
        in_specs=[vmem] * 10 + [smem] * 2,
        out_specs=[vmem] * 4,
        scratch_shapes=[pltpu.VMEM((n, length, features), BF16)] * 4
        + [pltpu.VMEM((n, features, states), F32)] * 2
        + [pltpu.VMEM((features, states), F32)] * 2,
        name="compute",
    )(u, w1, r1, w2, r2, g1, g2, o1, o2, ct, k1, k2)


def exchange_out_kernel(n, clips, factor, *refs):
    (du, params, decays, skips) = refs[:4]
    (dinput, dw1, dr1, dw2, dr2, dg1, dg2, dk1, dk2) = refs[4:13]
    (params_in, decays_in, clips_in, summed, parts_in, send, recv, clip_send, clip_recv) = refs[13:]
    me, clip = lax.axis_index("seq"), lax.axis_index("dp")
    width = du.shape[2]
    heads = decays.shape[2]
    size = width // heads
    barrier = pltpu.get_barrier_semaphore()
    for d in range(1, n):
        pl.semaphore_signal(barrier, inc=1, device_id={"seq": lax.rem(me + d, n)}, device_id_type=MESH)
    for d in range(1, clips):
        pl.semaphore_signal(barrier, inc=1, device_id={"dp": lax.rem(clip + d, clips)}, device_id_type=MESH)
    pl.semaphore_wait(barrier, n + clips - 2)

    def send_to(axis, to, src, dst, one, two):
        copy = pltpu.make_async_remote_copy(
            src_ref=src, dst_ref=dst, send_sem=one, recv_sem=two, device_id={axis: to}, device_id_type=MESH
        )
        copy.start()
        return copy

    clip_copies = []
    for d in range(1, clips):
        to = lax.rem(clip + d, clips)
        clip_copies.append(send_to("dp", to, skips, clips_in.at[clip], clip_send.at[d - 1], clip_recv.at[d - 1]))
    here = pl.ds(pl.multiple_of(me * width, width), width)
    copies = []
    for d in range(1, n):
        to = lax.rem(me + d, n)
        for k, (src, dst) in enumerate(
            [(params.at[to], params_in.at[me]), (decays.at[to], decays_in.at[me]), (du.at[to], dinput.at[:, here])]
        ):
            copies.append(send_to("seq", to, src, dst, send.at[d - 1, k], recv.at[d - 1, k]))
    clips_in[clip] = skips[...]
    params_in[me] = params[me]
    decays_in[me] = decays[me]
    dinput[:, here] = du[me]
    for copy in clip_copies:
        copy.wait()
    summed[...] = jnp.sum(clips_in[...], axis=0)
    parts_in[me] = summed[...]
    for d in range(1, n):
        to = lax.rem(me + d, n)
        copies.append(send_to("seq", to, summed, parts_in.at[me], send.at[d - 1, 3], recv.at[d - 1, 3]))
    for copy in copies:
        copy.wait()
    for k, out in enumerate((dw1, dr1, dw2, dr2)):
        total = params_in[0, k].astype(F32)
        for s in range(1, n):
            total = total + params_in[s, k].astype(F32)
        out[...] = total.astype(BF16)
    picks = (iota((width, heads), 0) // size == iota((width, heads), 1)).astype(F32)
    for s in range(n):
        dg1[s] = decays_in[s, 0]
        dg2[s] = decays_in[s, 1]
        by_head = nn(parts_in[s], picks, HIGHEST) * factor
        dk1[:, s * heads : (s + 1) * heads] = by_head[0:1]
        dk2[:, s * heads : (s + 1) * heads] = by_head[1:2]


def exchange_out(n, clips, factor, du, params, decays, skips):
    _, length, features = du.shape
    states = params.shape[3]
    heads = decays.shape[2]
    vmem = pl.BlockSpec(memory_space=pltpu.VMEM)
    param = jax.ShapeDtypeStruct((length, states), BF16)
    decay = jax.ShapeDtypeStruct((n, heads, length), F32)
    skip = jax.ShapeDtypeStruct((1, n * heads), F32)
    return pl.pallas_call(
        functools.partial(exchange_out_kernel, n, clips, factor),
        out_shape=(jax.ShapeDtypeStruct((length, n * features), BF16),) + (param,) * 4 + (decay,) * 2 + (skip,) * 2,
        in_specs=[vmem] * 4,
        out_specs=[vmem] * 9,
        scratch_shapes=[
            pltpu.VMEM(params.shape, params.dtype),
            pltpu.VMEM(decays.shape, F32),
            pltpu.VMEM((clips, 2, features), F32),
            pltpu.VMEM((2, features), F32),
            pltpu.VMEM((n, 2, features), F32),
            pltpu.SemaphoreType.DMA((n - 1, 4)),
            pltpu.SemaphoreType.DMA((n - 1, 4)),
            pltpu.SemaphoreType.DMA((clips - 1,)),
            pltpu.SemaphoreType.DMA((clips - 1,)),
        ],
        compiler_params=pltpu.CompilerParams(collective_id=1, has_side_effects=True),
        name="exchange_out",
    )(du, params, decays, skips)


def on_device(n, clips, u, w1, r1, g1, k1, w2, r2, g2, k2, o1, o2, ct):
    length, features = u.shape[1:]
    head_count = k1.shape[0]
    size = features // head_count
    heads = head_count // n

    def by_device(g):
        return g.reshape(n, heads, length)

    arrived = exchange_in(
        n, u[0], w1[0], r1[0], w2[0], r2[0], by_device(g1), by_device(g2), o1[None], o2[None], ct[0]
    )
    results = compute(n, size, *arrived, k1, k2)
    factor = 1.0 / math.sqrt(clips * n * length * size)
    du, dw1, dr1, dw2, dr2, dg1, dg2, dk1, dk2 = exchange_out(n, clips, factor, *results)
    return (
        du[None],
        dw1[None],
        dr1[None],
        dg1.reshape(1, head_count, length),
        dk1[0],
        dw2[None],
        dr2[None],
        dg2.reshape(1, head_count, length),
        dk2[0],
    )


def solution(mesh):
    tokens, decay = P("dp", "seq", None), P("dp", None, "seq")
    return jax.shard_map(
        functools.partial(on_device, mesh.shape["seq"], mesh.shape["dp"]),
        mesh=mesh,
        in_specs=(tokens, tokens, tokens, decay, P(), tokens, tokens, decay, P(), P("seq"), P("seq"), tokens),
        out_specs=(tokens, tokens, tokens, decay, P(), tokens, tokens, decay, P()),
        check_vma=False,
    )
```

profile of v0, /device:TPU:0, one launch (start us, length us, event | category | flops | bytes accessed | tf_op | source)
XLA Modules:
  0.0 76.1 jit_solution(10509506467627471343)
XLA Ops:
  0.6 24.0 %exchange_in.1 = (bf16[4,128,512]{2,1,0:T(8,128)(2,1)}, bf16[4,128,128]{2,1,0:T(8,128)(2,1)}, bf16[4,128,128]{2,1,0:T(8,128)(2,1)}, bf16[4,128,128]{2,1,0:T(8,12...) custom-call(bf16[128,2048]{1,0:T(8,128)(2,1)} %bitcast.20, ...), custom_call_target="tpu_custom_call" | custom-call | tf_op jit(solution)/shard_map/exchange_in/pallas_call | solution.py:98
  24.6 23.1 %compute.1 = (bf16[4,128,512]{2,1,0:T(8,128)(2,1)}, bf16[4,4,128,128]{3,2,1,0:T(8,128)(2,1)}, f32[4,2,8,128]{3,2,1,0:T(8,128)}, f32[2,512]{1,0:T(2,128)}) custom-call(bf16[4,128,512]{2,1,0:T(8,128)(2,1)} %get-tuple-element.32.refs_0_, bf16[4,128,128]{2,1,0:T(8,128)(2,1)} %get-tuple-element.33.refs_1_, bf16[4,128,128]{2,1,0:T(8,128)(2,1)} %get-tuple-element.34.refs_2_, ...), custom_call_target="tpu_custom_call" | custom-call | tf_op jit(solution)/shard_map/compute/pallas_call | solution.py:344
  47.8 21.2 %exchange_out.1 = (bf16[128,2048]{1,0:T(8,128)(2,1)}, bf16[128,128]{1,0:T(8,128)(2,1)}, bf16[128,128]{1,0:T(8,128)(2,1)}, bf16[128,128]{1,0:T(8,128)(2,1)}, bf16...) custom-call(bf16[4,128,512]{2,1,0:T(8,128)(2,1)} %get-tuple-element., ...), custom_call_target="tpu_custom_call" | custom-call | tf_op jit(solution)/shard_map/exchange_out/pallas_call | solution.py:430
  69.0 0.0 copy-start.3
  69.0 1.9 %copy.30 = bf16[1,128,2048]{2,1,0:T(8,128)(2,1)} copy(bf16[1,128,2048]{2,1,0:T(8,128)(2,1)} %bitcast.21) | data formatting | bytes 1048576
  70.9 0.0 copy-done.3
  70.9 0.0 copy-start.2
  70.9 0.6 copy.31
  71.5 0.2 copy-done.2
  71.6 0.0 copy-start.5
  71.7 0.0 copy-start.7
  71.7 0.6 copy.32
  72.3 0.1 copy-done.5
  72.4 0.6 copy.33
  73.0 0.0 copy-done.7
  73.0 0.5 copy.34
  73.5 0.0 copy-done.1
  73.5 0.6 copy.35
  74.1 0.2 copy-done
  74.3 0.6 copy.36
  74.9 0.1 copy-done.4
  75.0 0.6 copy.37
  75.6 0.0 copy-done.6
  75.6 0.5 copy.38
  (4 shorter events, 0.0 us)
Async XLA Ops:
  69.0 1.9 %copy-start.3 = (bf16[128,128]{1,0:T(8,128)(2,1)S(1)}, bf16[128,128]{1,0:T(8,128)(2,1)}, u32[]{:S(2)}) copy-start(bf16[128,128]{1,0:T(8,128)(2,1)} %get-tuple-element.47) | copy-start | bytes 98308
  70.9 0.8 %copy-start.2 = (bf16[128,128]{1,0:T(8,128)(2,1)S(1)}, bf16[128,128]{1,0:T(8,128)(2,1)}, u32[]{:S(2)}) copy-start(bf16[128,128]{1,0:T(8,128)(2,1)} %get-tuple-element.48) | copy-start | bytes 98308
  71.6 0.7 copy-start.5
  71.7 1.3 %copy-start.7 = (f32[1,32]{1,0:T(1,128)S(1)}, f32[1,32]{1,0:T(1,128)}, u32[]{:S(2)}) copy-start(f32[1,32]{1,0:T(1,128)} %get-tuple-element.50) | copy-start | bytes 388
  72.4 1.1 %copy-start.1 = (bf16[128,128]{1,0:T(8,128)(2,1)S(1)}, bf16[128,128]{1,0:T(8,128)(2,1)}, u32[]{:S(2)}) copy-start(bf16[128,128]{1,0:T(8,128)(2,1)} %get-tuple-element.51) | copy-start | bytes 98308
  73.5 0.8 %copy-start = (bf16[128,128]{1,0:T(8,128)(2,1)S(1)}, bf16[128,128]{1,0:T(8,128)(2,1)}, u32[]{:S(2)}) copy-start(bf16[128,128]{1,0:T(8,128)(2,1)} %get-tuple-element.52) | copy-start | bytes 98308
  74.3 0.7 copy-start.4
  75.0 0.6 copy-start.6
where the time goes:
time: 76.6 us; the launch traced here: 76.1 us
  Pallas kernels  68.3 us (89%)
  local copies, waits for them, and re-layouts  7.13 us (9%)
    pallas_call x1, Pallas kernels, exchange_in(): pl.pallas_call(functools.partial(exchange_in_kernel, n, heads), out_shape...  24 us
    pallas_call x1, Pallas kernels, compute(): pl.pallas_call(functools.partial(compute_kernel, n, size), out_shape=(jax...  23.1 us
    pallas_call x1, Pallas kernels, exchange_out(): pl.pallas_call(functools.partial(exchange_out_kernel, n, clips, factor),...  21.2 us
    unnamed x25, local copies, waits for them, and re-layouts  7.13 us

commit v1 on v0

v1 whole, which is shorter than its diff:
```python
import functools
import math

import jax
import jax.numpy as jnp
from jax import lax
from jax.experimental import pallas as pl
from jax.experimental.pallas import tpu as pltpu
from jax.sharding import PartitionSpec as P

MESH = pl.DeviceIdType.MESH
HIGHEST = lax.Precision.HIGHEST
F32 = jnp.float32
BF16 = jnp.bfloat16


def nn(a, b, precision=None):
    return lax.dot_general(a, b, (((1,), (0,)), ((), ())), precision=precision, preferred_element_type=F32)


def nt(a, b, precision=None):
    return lax.dot_general(a, b, (((1,), (1,)), ((), ())), precision=precision, preferred_element_type=F32)


def tn(a, b, precision=None):
    return lax.dot_general(a, b, (((0,), (0,)), ((), ())), precision=precision, preferred_element_type=F32)


def iota(shape, dim):
    return lax.broadcasted_iota(jnp.int32, shape, dim)


def two(a):
    high = a.astype(BF16)
    return high, (a - high.astype(F32)).astype(BF16)


def nn2(a, b):
    high, low = two(a)
    return nn(high, b) + nn(low, b)


def nt2(a, b):
    high, low = two(b)
    return nt(a, high) + nt(a, low)


def tn2(a, b):
    high, low = two(a)
    return tn(high, b) + tn(low, b)


def spread(x, size):
    per = 128 // size
    rows, heads = x.shape
    lane = iota((rows, 128), 1) // size
    parts = []
    for j in range(heads // per):
        part = jnp.broadcast_to(x[:, per * j : per * j + 1], (rows, 128))
        for k in range(1, per):
            part = jnp.where(lane == k, x[:, per * j + k : per * j + k + 1], part)
        parts.append(part)
    return jnp.concatenate(parts, axis=1)


def split_heads(x, size):
    lane = iota(x.shape, 1) // size
    return jnp.concatenate([jnp.where(lane == k, x, jnp.zeros_like(x)) for k in range(128 // size)], axis=0)


def scale_rows(state, factor, size):
    heads = factor.shape[0]
    return jnp.concatenate(
        [state[h * size : (h + 1) * size] * factor[h : h + 1] for h in range(heads)], axis=0
    )


class Chunk:
    def __init__(self, log_decay, size):
        heads, length = log_decay.shape
        self.size, self.heads, self.length = size, heads, length
        before = (iota((length, length), 0) <= iota((length, length), 1)).astype(F32)
        after = (iota((length, length), 1) <= iota((length, length), 0)).astype(F32)
        self.row = nn(log_decay, before, HIGHEST)
        self.col = nt(after, log_decay, HIGHEST)
        total = self.col[length - 1 : length, :]
        self.grown = jnp.exp(self.col)
        self.left = jnp.exp(total - self.col)
        self.total = jnp.exp(self.row[:, length - 1 : length])

    def gaps(self, h):
        gap = self.col[:, h : h + 1] - self.row[h : h + 1, :]
        causal = iota(gap.shape, 0) >= iota(gap.shape, 1)
        return jnp.where(causal, jnp.exp(jnp.minimum(gap, 0.0)), 0.0)

    def gaps_turned(self, h):
        gap = self.row[h : h + 1, :] - self.col[:, h : h + 1]
        causal = iota(gap.shape, 0) <= iota(gap.shape, 1)
        return jnp.where(causal, jnp.exp(jnp.minimum(gap, 0.0)), 0.0)


def layer_forward(u, w, r, chunk, skip, state):
    size = chunk.size
    per = 128 // size
    scores = nt(r, w)
    outputs = []
    for j in range(chunk.heads // per):
        weights = jnp.concatenate(
            [chunk.gaps(per * j + k) * scores for k in range(per)], axis=1
        )
        outputs.append(nn2(weights, split_heads(u[:, 128 * j : 128 * (j + 1)], size)))
    wide = u.astype(F32)
    y = jnp.concatenate(outputs, axis=1) + spread(chunk.grown, size) * nt2(r, state) + skip * wide
    scaled = wide * spread(chunk.left, size)
    return y, scale_rows(state, chunk.total, size) + tn2(scaled, w)


def layer_back(dy, w, r, chunk, skip, adjoint):
    size = chunk.size
    per = 128 // size
    scores = nt(w, r)
    outputs = []
    for j in range(chunk.heads // per):
        weights = jnp.concatenate(
            [chunk.gaps_turned(per * j + k) * scores for k in range(per)], axis=1
        )
        outputs.append(nn2(weights, split_heads(dy[:, 128 * j : 128 * (j + 1)], size)))
    wide = dy.astype(F32)
    du = jnp.concatenate(outputs, axis=1) + spread(chunk.left, size) * nt2(w, adjoint) + skip * wide
    scaled = wide * spread(chunk.grown, size)
    return du, scale_rows(adjoint, chunk.total, size) + tn2(scaled, r)


def layer_grads(u, dy, w, r, chunk, skip, state, adjoint, want_input):
    size, heads, length = chunk.size, chunk.heads, chunk.length
    per = 128 // size
    features = heads * size
    scores = nt(w, r)
    since = (iota((length, length), 0) >= iota((length, length), 1)).astype(BF16)
    earlier = iota((length, length), 0) < iota((length, length), 1)
    picks = (iota((heads, features), 1) // size == iota((heads, features), 0)).astype(BF16)
    dscores = jnp.zeros((length, length), F32)
    rows, outputs = [], []
    for j in range(heads // per):
        lanes = slice(128 * j, 128 * (j + 1))
        crossed = nt(split_heads(u[:, lanes], size), dy[:, lanes])
        moved, weights = [], []
        for k in range(per):
            gap = chunk.gaps_turned(per * j + k)
            part = gap * crossed[k * length : (k + 1) * length]
            dscores = dscores + part
            moved.append((part * scores).astype(BF16))
            if want_input:
                weights.append((gap * scores).astype(BF16))
        sums = nn(jnp.concatenate(moved, axis=0), since)
        for k in range(per):
            rows.append(
                jnp.sum(
                    jnp.where(earlier, sums[k * length : (k + 1) * length], 0.0), axis=0, keepdims=True
                )
            )
        if want_input:
            outputs.append(nn(jnp.concatenate(weights, axis=1), split_heads(dy[:, lanes], size)))
    wide_u, wide_dy = u.astype(F32), dy.astype(F32)
    left = spread(chunk.left, size)
    dy_scaled = wide_dy * spread(chunk.grown, size)
    u_scaled = wide_u * left
    dy_low, u_low = dy_scaled.astype(BF16), u_scaled.astype(BF16)
    state_low, adjoint_low = state.astype(BF16), adjoint.astype(BF16)
    dscores = dscores.astype(BF16)
    dreads = tn(dscores, w) + nn(dy_low, state_low)
    dwrites = nn(dscores, r) + nn(u_low, adjoint_low)
    read = nt(r, state_low)
    back = nt(w, adjoint_low)
    come = nt(picks, (dy_scaled * read).astype(BF16))
    gone = nt(picks, (u_scaled * back).astype(BF16))
    through = jnp.sum(nn(picks, (state * adjoint).astype(BF16)), axis=1, keepdims=True) * chunk.total
    ddecay = (
        jnp.concatenate(rows, axis=0)
        + nn(come.astype(BF16), since)
        + nn(gone.astype(BF16), earlier.astype(BF16))
        + through
    )
    if want_input:
        du = jnp.concatenate(outputs, axis=1) + left * back + skip * wide_dy
        return dwrites, dreads, ddecay, du, scale_rows(adjoint, chunk.total, size) + tn(dy_low, r)
    return dwrites, dreads, ddecay, None, scale_rows(state, chunk.total, size) + tn(u_low, w)


def whole_kernel(n, clips, size, *refs):
    (u, w1, r1, g1, k1, w2, r2, g2, k2, o1, o2, ct) = refs[:12]
    (dinput, params1_in, params2_in, decays1_in, decays2_in, parts_in) = refs[12:18]
    (u1, w1_all, r1_all, g1_all, w2_all, r2_all, g2_all, o1_all, o2_all, ct_high, ct_low) = refs[18:29]
    (high_out, low_out, y1, du2_high, du2, u2, dy1, states, adjoints, state, adjoint) = refs[29:40]
    (du1, params1, params2, decays1, decays2, skips, clips_in, summed) = refs[40:48]
    (send, recv, out_send, out_recv, clip_send, clip_recv) = refs[48:]
    me, clip = lax.axis_index("seq"), lax.axis_index("dp")
    heads, length = g1.shape[1:]
    features = heads * size
    here = pl.ds(pl.multiple_of(me * features, features), features)

    barrier = pltpu.get_barrier_semaphore()
    for d in range(1, n):
        pl.semaphore_signal(barrier, inc=1, device_id={"seq": lax.rem(me + d, n)}, device_id_type=MESH)
    for d in range(1, clips):
        pl.semaphore_signal(barrier, inc=1, device_id={"dp": lax.rem(clip + d, clips)}, device_id_type=MESH)
    high, low = two(ct[...])
    high_out[...] = high
    low_out[...] = low
    pl.semaphore_wait(barrier, n + clips - 2)

    def copy_to(axis, to, src, dst, one, other):
        return pltpu.make_async_remote_copy(
            src_ref=src, dst_ref=dst, send_sem=one, recv_sem=other, device_id={axis: to}, device_id_type=MESH
        )

    def cut(ref, at):
        return ref.at[:, pl.ds(pl.multiple_of(at * features, features), features)]

    moves = [
        lambda to: (g2.at[to], g2_all.at[me]),
        lambda to: (w2, w2_all.at[me]),
        lambda to: (r2, r2_all.at[me]),
        lambda to: (cut(high_out, to), ct_high.at[me]),
        lambda to: (g1.at[to], g1_all.at[me]),
        lambda to: (w1, w1_all.at[me]),
        lambda to: (r1, r1_all.at[me]),
        lambda to: (cut(u, to), u1.at[me]),
        lambda to: (o1, o1_all.at[me]),
        lambda to: (o2, o2_all.at[me]),
        lambda to: (cut(low_out, to), ct_low.at[me]),
    ]
    arriving = []
    for k, move in enumerate(moves):
        arriving.append([])
        for d in range(1, n):
            to = lax.rem(me + d, n)
            src, dst = move(to)
            copy = copy_to("seq", to, src, dst, send.at[d - 1, k], recv.at[d - 1, k])
            copy.start()
            arriving[k].append(copy)
    for src, dst in ((g1, g1_all), (g2, g2_all)):
        dst[me] = src[me]
    for src, dst in ((w1, w1_all), (r1, r1_all), (w2, w2_all), (r2, r2_all), (o1, o1_all), (o2, o2_all)):
        dst[me] = src[...]
    u1[me] = u[:, here]
    ct_high[me] = high_out[:, here]
    ct_low[me] = low_out[:, here]

    first = me * heads

    def gains(ref):
        channel = iota((1, features), 1) // size
        row = jnp.zeros((1, features), F32)
        for h in range(heads):
            row = jnp.where(channel == h, ref[first + h], row)
        return row

    skip1, skip2 = gains(k1), gains(k2)
    state[...] = jnp.zeros_like(state)
    adjoint[...] = jnp.zeros_like(adjoint)

    for k in range(0, 4):
        for copy in arriving[k]:
            copy.wait_recv()

    def back_second(i, carry):
        b = n - 1 - i
        adjoints[b] = adjoint[...]
        du, new = layer_back(ct_high[b], w2_all[b], r2_all[b], Chunk(g2_all[b], size), skip2, adjoint[...])
        du2_high[b] = du
        adjoint[...] = new
        return carry

    lax.fori_loop(0, n, back_second, 0)
    for k in range(4, 8):
        for copy in arriving[k]:
            copy.wait_recv()

    def forward_first(i, carry):
        states[i] = state[...]
        y, new = layer_forward(u1[i], w1_all[i], r1_all[i], Chunk(g1_all[i], size), skip1, state[...])
        y1[i] = y.astype(BF16)
        state[...] = new
        return carry

    lax.fori_loop(0, n, forward_first, 0)
    for k in range(8, 11):
        for copy in arriving[k]:
            copy.wait_recv()

    def finish_back(i, carry):
        du2[i] = (du2_high[i] + skip2 * ct_low[i].astype(F32)).astype(BF16)
        return carry

    lax.fori_loop(0, n, finish_back, 0)
    skips[...] = jnp.zeros_like(skips)

    def regrid(i, carry):
        second = jnp.transpose(jnp.broadcast_to(o2_all[i].astype(F32), (length, length)))
        first_cells = jnp.transpose(jnp.broadcast_to(o1_all[i].astype(F32), (length, length)))
        forward = jnp.zeros((length, features), F32)
        back = jnp.zeros((length, features), F32)
        for j in range(n):
            take = (second == o1_all[j].astype(F32)).astype(BF16)
            forward = forward + nn(take, y1[j])
            take = (first_cells == o2_all[j].astype(F32)).astype(BF16)
            back = back + nn(take, du2[j])
        u2[i] = forward.astype(BF16)
        dy1[i] = back.astype(BF16)
        upstream = ct_high[i].astype(F32) + ct_low[i].astype(F32)
        skips[0:1, :] += jnp.sum(u1[i].astype(F32) * back, axis=0, keepdims=True)
        skips[1:2, :] += jnp.sum(upstream * forward, axis=0, keepdims=True)
        return carry

    lax.fori_loop(0, n, regrid, 0)
    clip_copies = []
    for d in range(1, clips):
        to = lax.rem(clip + d, clips)
        copy = copy_to("dp", to, skips, clips_in.at[clip], clip_send.at[d - 1], clip_recv.at[d - 1])
        copy.start()
        clip_copies.append(copy)
    clips_in[clip] = skips[...]
    state[...] = jnp.zeros_like(state)
    adjoint[...] = jnp.zeros_like(adjoint)

    def leave_second(to, slot):
        return [
            copy_to("seq", to, params2.at[to], params2_in.at[me], out_send.at[slot, 0], out_recv.at[slot, 0]),
            copy_to("seq", to, decays2.at[to], decays2_in.at[me], out_send.at[slot, 1], out_recv.at[slot, 1]),
        ]

    def leave_first(to, slot):
        return [
            copy_to("seq", to, du1.at[to], dinput.at[:, here], out_send.at[slot, 2], out_recv.at[slot, 2]),
            copy_to("seq", to, params1.at[to], params1_in.at[me], out_send.at[slot, 3], out_recv.at[slot, 3]),
            copy_to("seq", to, decays1.at[to], decays1_in.at[me], out_send.at[slot, 4], out_recv.at[slot, 4]),
        ]

    def grads(i, carry):
        b = n - 1 - i
        dw, dr, dg, _, new = layer_grads(
            u2[i], ct_high[i], w2_all[i], r2_all[i], Chunk(g2_all[i], size), skip2, state[...], adjoints[i], False
        )
        state[...] = new
        params2[i, 0] = dw.astype(BF16)
        params2[i, 1] = dr.astype(BF16)
        decays2[i] = dg

        @pl.when(i != me)
        def _():
            for copy in leave_second(i, lax.rem(i - me + n, n) - 1):
                copy.start()

        dw, dr, dg, du, new = layer_grads(
            u1[b], dy1[b], w1_all[b], r1_all[b], Chunk(g1_all[b], size), skip1, states[b], adjoint[...], True
        )
        adjoint[...] = new
        du1[b] = du.astype(BF16)
        params1[b, 0] = dw.astype(BF16)
        params1[b, 1] = dr.astype(BF16)
        decays1[b] = dg

        @pl.when(b != me)
        def _():
            for copy in leave_first(b, lax.rem(b - me + n, n) - 1):
                copy.start()

        return carry

    lax.fori_loop(0, n, grads, 0)
    for copy in clip_copies:
        copy.wait()
    summed[...] = jnp.sum(clips_in[...], axis=0)
    last = []
    for d in range(1, n):
        to = lax.rem(me + d, n)
        copy = copy_to("seq", to, summed, parts_in.at[me], out_send.at[d - 1, 5], out_recv.at[d - 1, 5])
        copy.start()
        last.append(copy)
    parts_in[me] = summed[...]
    params1_in[me] = params1[me]
    params2_in[me] = params2[me]
    decays1_in[me] = decays1[me]
    decays2_in[me] = decays2[me]
    dinput[:, here] = du1[me]
    for group in arriving:
        for copy in group:
            copy.wait_send()
    for d in range(1, n):
        to = lax.rem(me + d, n)
        last += leave_second(to, d - 1) + leave_first(to, d - 1)
    for copy in last:
        copy.wait()


def whole(n, clips, size, u, w1, r1, g1, k1, w2, r2, g2, k2, o1, o2, ct):
    length, width = u.shape
    heads = g1.shape[1]
    count = w1.shape[1]
    features = heads * size
    vmem = pl.BlockSpec(memory_space=pltpu.VMEM)
    smem = pl.BlockSpec(memory_space=pltpu.SMEM)
    wide, param, params = (n, length, features), (n, length, count), (n, 2, length, count)
    decay, order, gain = (n, heads, length), (n, 1, length), (2, features)
    outs = (((length, width), BF16), (params, BF16), (params, BF16), (decay, F32), (decay, F32), ((n,) + gain, F32))
    held = [
        (wide, BF16),
        (param, BF16),
        (param, BF16),
        (decay, F32),
        (param, BF16),
        (param, BF16),
        (decay, F32),
        (order, jnp.int32),
        (order, jnp.int32),
        (wide, BF16),
        (wide, BF16),
        ((length, width), BF16),
        ((length, width), BF16),
        (wide, BF16),
        (wide, F32),
        (wide, BF16),
        (wide, BF16),
        (wide, BF16),
        ((n, features, count), F32),
        ((n, features, count), F32),
        ((features, count), F32),
        ((features, count), F32),
        (wide, BF16),
        (params, BF16),
        (params, BF16),
        (decay, F32),
        (decay, F32),
        (gain, F32),
        ((clips,) + gain, F32),
        (gain, F32),
    ]
    return pl.pallas_call(
        functools.partial(whole_kernel, n, clips, size),
        out_shape=tuple(jax.ShapeDtypeStruct(*out) for out in outs),
        in_specs=[vmem] * 4 + [smem] + [vmem] * 3 + [smem] + [vmem] * 3,
        out_specs=[vmem] * 6,
        scratch_shapes=[pltpu.VMEM(*one) for one in held]
        + [pltpu.SemaphoreType.DMA((n - 1, 11))] * 2
        + [pltpu.SemaphoreType.DMA((n - 1, 6))] * 2
        + [pltpu.SemaphoreType.DMA((clips - 1,))] * 2,
        compiler_params=pltpu.CompilerParams(collective_id=0, has_side_effects=True),
        name="whole",
    )(u, w1, r1, g1, k1, w2, r2, g2, k2, o1, o2, ct)


def gather_kernel(n, factor, *refs):
    (du, params1, params2, decays1, decays2, parts) = refs[:6]
    (dinput, dw1, dr1, dg1, dk1, dw2, dr2, dg2, dk2) = refs[6:]
    heads = decays1.shape[1]
    width = parts.shape[2]
    size = width // heads
    dinput[...] = du[...]
    dg1[...] = decays1[...]
    dg2[...] = decays2[...]
    for params, outs in ((params1, (dw1, dr1)), (params2, (dw2, dr2))):
        for k, out in enumerate(outs):
            total = params[0, k].astype(F32)
            for s in range(1, n):
                total = total + params[s, k].astype(F32)
            out[...] = total.astype(BF16)
    picks = (iota((width, heads), 0) // size == iota((width, heads), 1)).astype(F32)
    for s in range(n):
        by_head = nn(parts[s], picks, HIGHEST) * factor
        dk1[:, s * heads : (s + 1) * heads] = by_head[0:1]
        dk2[:, s * heads : (s + 1) * heads] = by_head[1:2]


def gather(n, factor, du, params1, params2, decays1, decays2, parts):
    length, count = params1.shape[2:]
    heads = decays1.shape[1]
    vmem = pl.BlockSpec(memory_space=pltpu.VMEM)
    param = jax.ShapeDtypeStruct((length, count), BF16)
    decay = jax.ShapeDtypeStruct(decays1.shape, F32)
    skip = jax.ShapeDtypeStruct((1, n * heads), F32)
    layer = (param, param, decay, skip)
    return pl.pallas_call(
        functools.partial(gather_kernel, n, factor),
        out_shape=(jax.ShapeDtypeStruct(du.shape, BF16),) + layer + layer,
        in_specs=[vmem] * 6,
        out_specs=[vmem] * 9,
        name="gather",
    )(du, params1, params2, decays1, decays2, parts)


def on_device(n, clips, u, w1, r1, g1, k1, w2, r2, g2, k2, o1, o2, ct):
    length, features = u.shape[1:]
    head_count = k1.shape[0]
    size = features // head_count
    heads = head_count // n

    def by_device(g):
        return g.reshape(n, heads, length)

    results = whole(
        n,
        clips,
        size,
        u[0],
        w1[0],
        r1[0],
        by_device(g1),
        k1,
        w2[0],
        r2[0],
        by_device(g2),
        k2,
        o1[None],
        o2[None],
        ct[0],
    )
    factor = 1.0 / math.sqrt(clips * n * length * size)
    du, dw1, dr1, dg1, dk1, dw2, dr2, dg2, dk2 = gather(n, factor, *results)
    return (
        du[None],
        dw1[None],
        dr1[None],
        dg1.reshape(1, head_count, length),
        dk1[0],
        dw2[None],
        dr2[None],
        dg2.reshape(1, head_count, length),
        dk2[0],
    )


def solution(mesh):
    tokens, decay = P("dp", "seq", None), P("dp", None, "seq")
    return jax.shard_map(
        functools.partial(on_device, mesh.shape["seq"], mesh.shape["dp"]),
        mesh=mesh,
        in_specs=(tokens, tokens, tokens, decay, P(), tokens, tokens, decay, P(), P("seq"), P("seq"), tokens),
        out_specs=(tokens, tokens, tokens, decay, P(), tokens, tokens, decay, P()),
        check_vma=False,
    )
```

time: 76.6 us -> 58.1 us (0.76)
  Pallas kernels: 68.3 us -> 57.3 us
  local copies, waits for them, and re-layouts: 7.13 us -> 0 us
    pallas_call x3 -> x2, Pallas kernels: 68.3 us -> 57.3 us  [the longest x1 54.6 us: whole(): pl.pallas_call(functools.partial(whole_kernel, n, clips, size), out_shape...]
    unnamed x25 -> x0, local copies, waits for them, and re-layouts: 7.13 us -> none
where the time goes in v1:
time: 58.1 us; the launch traced here: 57.9 us
  Pallas kernels  57.3 us (99%)
  between operations  0.65 us (1%)
    pallas_call x1, Pallas kernels, whole(): pl.pallas_call(functools.partial(whole_kernel, n, clips, size), out_shape...  54.6 us
    pallas_call x1, Pallas kernels, gather(): pl.pallas_call(functools.partial(gather_kernel, n, factor), out_shape=(ja...  2.62 us

profile of v1, /device:TPU:0, one launch (start us, length us, event | category | flops | bytes accessed | tf_op | source)
XLA Modules:
  0.0 57.9 jit_solution(12433823521888830345)
XLA Ops:
  0.6 54.6 %whole.1 = (bf16[128,2048]{1,0:T(8,128)(2,1)}, bf16[4,2,128,128]{3,2,1,0:T(8,128)(2,1)}, bf16[4,2,128,128]{3,2,1,0:T(8,128)(2,1)}, f32[4,8,128]{2,1,0:T(8,128)},...) custom-call(bf16[128,2048]{1,0:T(8,128)(2,1)} %bitcast.20, bf16[128,128]{1,0:T(8,128)(2,1)} %bitcast.21, ...), custom_call_target="tpu_custom_call" | custom-call | tf_op jit(solution)/shard_map/whole/pallas_call | solution.py:439
  55.3 2.6 %gather.1 = (bf16[128,2048]{1,0:T(8,128)(2,1)}, bf16[128,128]{1,0:T(8,128)(2,1)}, bf16[128,128]{1,0:T(8,128)(2,1)}, f32[4,8,128]{2,1,0:T(8,128)}, f32[1,32]{1,0:...) custom-call(bf16[128,2048]{1,0:T(8,128)(2,1)} %get-tuple-element.24.refs, ...), custom_call_target="tpu_custom_call" | custom-call | tf_op jit(solution)/shard_map/gather/pallas_call | solution.py:483

commit v2 on v1

--- a/solution.py
+++ b/solution.py
@@ -193,7 +193,7 @@
     (u1, w1_all, r1_all, g1_all, w2_all, r2_all, g2_all, o1_all, o2_all, ct_high, ct_low) = refs[18:29]
     (high_out, low_out, y1, du2_high, du2, u2, dy1, states, adjoints, state, adjoint) = refs[29:40]
     (du1, params1, params2, decays1, decays2, skips, clips_in, summed) = refs[40:48]
-    (send, recv, out_send, out_recv, clip_send, clip_recv) = refs[48:]
+    (send, recv, out_send, out_recv, clip_send, clip_recv, near_send, near_recv) = refs[48:]
     me, clip = lax.axis_index("seq"), lax.axis_index("dp")
     heads, length = g1.shape[1:]
     features = heads * size
@@ -219,17 +219,26 @@
 
     moves = [
         lambda to: (g2.at[to], g2_all.at[me]),
-        lambda to: (w2, w2_all.at[me]),
-        lambda to: (r2, r2_all.at[me]),
         lambda to: (cut(high_out, to), ct_high.at[me]),
         lambda to: (g1.at[to], g1_all.at[me]),
-        lambda to: (w1, w1_all.at[me]),
-        lambda to: (r1, r1_all.at[me]),
         lambda to: (cut(u, to), u1.at[me]),
         lambda to: (o1, o1_all.at[me]),
         lambda to: (o2, o2_all.at[me]),
         lambda to: (cut(low_out, to), ct_low.at[me]),
     ]
+    twin = me + 1 - 2 * lax.rem(me, 2)
+    pairs = ((w2, w2_all), (r2, r2_all), (w1, w1_all), (r1, r1_all))
+    far, near = [], []
+    for k, (src, dst) in enumerate(pairs):
+        for d in range(2, n, 2):
+            at = d // 2 - 1
+            copy = copy_to("seq", lax.rem(me + d, n), src, dst.at[me], near_send.at[at, k], near_recv.at[at, k])
+            copy.start()
+            far.append(copy)
+        at = n // 2 - 1
+        copy = copy_to("seq", twin, src, dst.at[me], near_send.at[at, k], near_recv.at[at, k])
+        copy.start()
+        near.append(copy)
     arriving = []
     for k, move in enumerate(moves):
         arriving.append([])
@@ -241,7 +250,7 @@
             arriving[k].append(copy)
     for src, dst in ((g1, g1_all), (g2, g2_all)):
         dst[me] = src[me]
-    for src, dst in ((w1, w1_all), (r1, r1_all), (w2, w2_all), (r2, r2_all), (o1, o1_all), (o2, o2_all)):
+    for src, dst in pairs + ((o1, o1_all), (o2, o2_all)):
         dst[me] = src[...]
     u1[me] = u[:, here]
     ct_high[me] = high_out[:, here]
@@ -260,7 +269,17 @@
     state[...] = jnp.zeros_like(state)
     adjoint[...] = jnp.zeros_like(adjoint)
 
-    for k in range(0, 4):
+    for copy in far:
+        copy.wait_recv()
+    for k, (src, dst) in enumerate(pairs):
+        for d in range(2, n, 2):
+            at, block = n // 2 + d // 2 - 1, lax.rem(me - d + n, n)
+            copy = copy_to("seq", twin, dst.at[block], dst.at[block], near_send.at[at, k], near_recv.at[at, k])
+            copy.start()
+            near.append(copy)
+    for copy in near:
+        copy.wait_recv()
+    for k in range(0, 2):
         for copy in arriving[k]:
             copy.wait_recv()
 
@@ -272,8 +291,8 @@
         adjoint[...] = new
         return carry
 
-    lax.fori_loop(0, n, back_second, 0)
-    for k in range(4, 8):
+    lax.fori_loop(0, n, back_second, 0, unroll=2)
+    for k in range(2, 4):
         for copy in arriving[k]:
             copy.wait_recv()
 
@@ -284,36 +303,82 @@
         state[...] = new
         return carry
 
-    lax.fori_loop(0, n, forward_first, 0)
-    for k in range(8, 11):
+    lax.fori_loop(0, n, forward_first, 0, unroll=2)
+    for k in range(4, 6):
         for copy in arriving[k]:
             copy.wait_recv()
 
-    def finish_back(i, carry):
-        du2[i] = (du2_high[i] + skip2 * ct_low[i].astype(F32)).astype(BF16)
-        return carry
-
-    lax.fori_loop(0, n, finish_back, 0)
-    skips[...] = jnp.zeros_like(skips)
+    def cells(ref, i):
+        return jnp.transpose(jnp.broadcast_to(ref[i].astype(F32), (length, length)))
 
     def regrid(i, carry):
-        second = jnp.transpose(jnp.broadcast_to(o2_all[i].astype(F32), (length, length)))
-        first_cells = jnp.transpose(jnp.broadcast_to(o1_all[i].astype(F32), (length, length)))
-        forward = jnp.zeros((length, features), F32)
-        back = jnp.zeros((length, features), F32)
+        second = cells(o2_all, i)
+        total = jnp.zeros((length, features), F32)
         for j in range(n):
             take = (second == o1_all[j].astype(F32)).astype(BF16)
-            forward = forward + nn(take, y1[j])
-            take = (first_cells == o2_all[j].astype(F32)).astype(BF16)
-            back = back + nn(take, du2[j])
-        u2[i] = forward.astype(BF16)
-        dy1[i] = back.astype(BF16)
-        upstream = ct_high[i].astype(F32) + ct_low[i].astype(F32)
-        skips[0:1, :] += jnp.sum(u1[i].astype(F32) * back, axis=0, keepdims=True)
-        skips[1:2, :] += jnp.sum(upstream * forward, axis=0, keepdims=True)
+            total = total + nn(take, y1[j])
+        u2[i] = total.astype(BF16)
         return carry
 
     lax.fori_loop(0, n, regrid, 0)
+
+    state[...] = jnp.zeros_like(state)
+    adjoint[...] = jnp.zeros_like(adjoint)
+
+    def leave_second(to, slot):
+        return [
+            copy_to("seq", to, params2.at[to], params2_in.at[me], out_send.at[slot, 0], out_recv.at[slot, 0]),
+            copy_to("seq", to, decays2.at[to], decays2_in.at[me], out_send.at[slot, 1], out_recv.at[slot, 1]),
+        ]
+
+    def leave_first(to, slot):
+        return [
+            copy_to("seq", to, du1.at[to], dinput.at[:, here], out_send.at[slot, 2], out_recv.at[slot, 2]),
+            copy_to("seq", to, params1.at[to], params1_in.at[me], out_send.at[slot, 3], out_recv.at[slot, 3]),
+            copy_to("seq", to, decays1.at[to], decays1_in.at[me], out_send.at[slot, 4], out_recv.at[slot, 4]),
+        ]
+
+    def grads_second(i, carry):
+        dw, dr, dg, _, new = layer_grads(
+            u2[i], ct_high[i], w2_all[i], r2_all[i], Chunk(g2_all[i], size), skip2, state[...], adjoints[i], False
+        )
+        state[...] = new
+        params2[i, 0] = dw.astype(BF16)
+        params2[i, 1] = dr.astype(BF16)
+        decays2[i] = dg
+
+        @pl.when(i != me)
+        def _():
+            for copy in leave_second(i, lax.rem(i - me + n, n) - 1):
+                copy.start()
+
+        return carry
+
+    lax.fori_loop(0, n, grads_second, 0)
+    for copy in arriving[6]:
+        copy.wait_recv()
+    skips[...] = jnp.zeros_like(skips)
+
+    def finish_back(i, carry):
+        rest = ct_low[i].astype(F32)
+        du2[i] = (du2_high[i] + skip2 * rest).astype(BF16)
+        upstream = ct_high[i].astype(F32) + rest
+        skips[1:2, :] += jnp.sum(upstream * u2[i].astype(F32), axis=0, keepdims=True)
+        return carry
+
+    lax.fori_loop(0, n, finish_back, 0)
+
+    def regrid_back(i, carry):
+        cell = cells(o1_all, i)
+        total = jnp.zeros((length, features), F32)
+        for j in range(n):
+            take = (cell == o2_all[j].astype(F32)).astype(BF16)
+            total = total + nn(take, du2[j])
+        dy1[i] = total.astype(BF16)
+        skips[0:1, :] += jnp.sum(u1[i].astype(F32) * total, axis=0, keepdims=True)
+        return carry
+
+    lax.fori_loop(0, n, regrid_back, 0)
     clip_copies = []
     for d in range(1, clips):
         to = lax.rem(clip + d, clips)
@@ -321,37 +386,9 @@
         copy.start()
         clip_copies.append(copy)
     clips_in[clip] = skips[...]
-    state[...] = jnp.zeros_like(state)
-    adjoint[...] = jnp.zeros_like(adjoint)
-
-    def leave_second(to, slot):
-        return [
-            copy_to("seq", to, params2.at[to], params2_in.at[me], out_send.at[slot, 0], out_recv.at[slot, 0]),
-            copy_to("seq", to, decays2.at[to], decays2_in.at[me], out_send.at[slot, 1], out_recv.at[slot, 1]),
-        ]
-
-    def leave_first(to, slot):
-        return [
-            copy_to("seq", to, du1.at[to], dinput.at[:, here], out_send.at[slot, 2], out_recv.at[slot, 2]),
-            copy_to("seq", to, params1.at[to], params1_in.at[me], out_send.at[slot, 3], out_recv.at[slot, 3]),
-            copy_to("seq", to, decays1.at[to], decays1_in.at[me], out_send.at[slot, 4], out_recv.at[slot, 4]),
-        ]
-
-    def grads(i, carry):
+
+    def grads_first(i, carry):
         b = n - 1 - i
-        dw, dr, dg, _, new = layer_grads(
-            u2[i], ct_high[i], w2_all[i], r2_all[i], Chunk(g2_all[i], size), skip2, state[...], adjoints[i], False
-        )
-        state[...] = new
-        params2[i, 0] = dw.astype(BF16)
-        params2[i, 1] = dr.astype(BF16)
-        decays2[i] = dg
-
-        @pl.when(i != me)
-        def _():
-            for copy in leave_second(i, lax.rem(i - me + n, n) - 1):
-                copy.start()
-
         dw, dr, dg, du, new = layer_grads(
             u1[b], dy1[b], w1_all[b], r1_all[b], Chunk(g1_all[b], size), skip1, states[b], adjoint[...], True
         )
@@ -368,7 +405,7 @@
 
         return carry
 
-    lax.fori_loop(0, n, grads, 0)
+    lax.fori_loop(0, n, grads_first, 0)
     for copy in clip_copies:
         copy.wait()
     summed[...] = jnp.sum(clips_in[...], axis=0)
@@ -387,6 +424,8 @@
     for group in arriving:
         for copy in group:
             copy.wait_send()
+    for copy in far + near:
+        copy.wait_send()
     for d in range(1, n):
         to = lax.rem(me + d, n)
         last += leave_second(to, d - 1) + leave_first(to, d - 1)
@@ -442,9 +481,10 @@
         in_specs=[vmem] * 4 + [smem] + [vmem] * 3 + [smem] + [vmem] * 3,
         out_specs=[vmem] * 6,
         scratch_shapes=[pltpu.VMEM(*one) for one in held]
-        + [pltpu.SemaphoreType.DMA((n - 1, 11))] * 2
+        + [pltpu.SemaphoreType.DMA((n - 1, 7))] * 2
         + [pltpu.SemaphoreType.DMA((n - 1, 6))] * 2
-        + [pltpu.SemaphoreType.DMA((clips - 1,))] * 2,
+        + [pltpu.SemaphoreType.DMA((clips - 1,))] * 2
+        + [pltpu.SemaphoreType.DMA((n - 1, 4))] * 2,
         compiler_params=pltpu.CompilerParams(collective_id=0, has_side_effects=True),
         name="whole",
     )(u, w1, r1, g1, k1, w2, r2, g2, k2, o1, o2, ct)

time: 58.1 us -> 56.1 us (0.966)
  Pallas kernels: 57.3 us -> 55.3 us
    pallas_call x1, Pallas kernels: 54.6 us -> 52.6 us  [whole(): pl.pallas_call(functools.partial(whole_kernel, n, clips, size), out_shape...]
where the time goes in v2:
time: 56.1 us; the launch traced here: 55.9 us
  Pallas kernels  55.3 us (99%)
  between operations  0.65 us (1%)
    pallas_call x1, Pallas kernels, whole(): pl.pallas_call(functools.partial(whole_kernel, n, clips, size), out_shape...  52.6 us
    pallas_call x1, Pallas kernels, gather(): pl.pallas_call(functools.partial(gather_kernel, n, factor), out_shape=(ja...  2.62 us

profile of v2, /device:TPU:0, one launch (start us, length us, event | category | flops | bytes accessed | tf_op | source)
XLA Modules:
  0.0 55.9 jit_solution(7156159079787352702)
XLA Ops:
  0.6 52.6 %whole.1 = (bf16[128,2048]{1,0:T(8,128)(2,1)}, bf16[4,2,128,128]{3,2,1,0:T(8,128)(2,1)}, bf16[4,2,128,128]{3,2,1,0:T(8,128)(2,1)}, f32[4,8,128]{2,1,0:T(8,128)},...) custom-call(bf16[128,2048]{1,0:T(8,128)(2,1)} %bitcast.20, bf16[128,128]{1,0:T(8,128)(2,1)} %bitcast.21, ...), custom_call_target="tpu_custom_call" | custom-call | tf_op jit(solution)/shard_map/whole/pallas_call | solution.py:478
  53.3 2.6 %gather.1 = (bf16[128,2048]{1,0:T(8,128)(2,1)}, bf16[128,128]{1,0:T(8,128)(2,1)}, bf16[128,128]{1,0:T(8,128)(2,1)}, f32[4,8,128]{2,1,0:T(8,128)}, f32[1,32]{1,0:...) custom-call(bf16[128,2048]{1,0:T(8,128)(2,1)} %get-tuple-element.24.refs, ...), custom_call_target="tpu_custom_call" | custom-call | tf_op jit(solution)/shard_map/gather/pallas_call | solution.py:523
